TPU v7x, 128 devices: a whole 4x4x4 slice. The times are simulated.
128 devices in a mesh: seq: 64 (over y_lo, x, z, core), head: 2 (over y_hi).
Axes of the slice: x: 4, y: 4 (y_hi: 2, y_lo: 2; y = y_hi * 2 + y_lo), z: 4, core: 2. Of those that a mesh axis runs over, the one named last changes fastest.
Arguments:
- queries: bfloat16 [32768, 768], P('seq', 'head'), may hold values from -7 to 7
- keys: bfloat16 [32768, 768], P('seq', 'head'), may hold values from -7 to 7
- values: bfloat16 [32768, 768], P('seq', 'head'), may hold values from -6 to 6
- w_out: bfloat16 [768, 768], P('head'), may hold values from -0.21875 to 0.21875
- d_out: bfloat16 [32768, 768], P('seq', 'head'), may hold values from -16 to 16
- slide_lengths: int32 [4], replicated, may hold values from 1 to 16384, 32768 in all
Outputs:
- out: bfloat16 [32768, 768], P('seq', 'head')
- d_queries: bfloat16 [32768, 768], P('seq', 'head')
- d_keys: bfloat16 [32768, 768], P('seq', 'head')
- d_values: bfloat16 [32768, 768], P('seq', 'head')
- d_w_out: float32 [768, 768], P('head', 'seq')
Inputs may be any that keep to these rules, and one draw needn't show every extreme that they name: `slide_lengths`: the lengths sum to 32768 and the longest is exactly 16384.
All inputs are finite; a program needn't handle non-finite values.
Results may differ from a plain program's by a relative error of at most 0.012.
Values may be sent and summed in bfloat16 or wider, within the bound.
A program may use at most 128 MiB of HBM per device.

v0:
```python
import jax
import jax.numpy as jnp
from jax import lax
from jax.experimental import pallas as pl
from jax.experimental.pallas import tpu as pltpu
from jax.sharding import PartitionSpec as P

TOKENS = 32768
HEAD = 48
ROWS = 512
WIDE = 384
HEADS = 8
NEG = -1e30
SCALE = HEAD**-0.5
LOG2E = 1.4426950408889634
C2 = SCALE * LOG2E
FAR = 1 << 30
F32 = jnp.float32
BF16 = jnp.bfloat16
MESH = pl.DeviceIdType.MESH


def nn(a, b):
    return lax.dot_general(a, b, (((1,), (0,)), ((), ())), preferred_element_type=F32)


def nt(a, b):
    return lax.dot_general(a, b, (((1,), (1,)), ((), ())), preferred_element_type=F32)


def tn(a, b):
    return lax.dot_general(a, b, (((0,), (0,)), ((), ())), preferred_element_type=F32)


def iota(shape, dim):
    return lax.broadcasted_iota(jnp.int32, shape, dim)


def token_of(a, g):
    return (a >> 7) + 4 * ((((a >> 5) & 3) + 2 * g) & 3) + 16 * ((a >> 3) & 3) + 64 * (a & 7)


def lane_head(rows):
    lane = iota((rows, WIDE), 1)
    head = jnp.zeros_like(lane)
    for i in range(1, HEADS):
        head = head + (lane >= HEAD * i).astype(jnp.int32)
    return head


def compact1(x):
    cls = lane_head(128) & 3
    y = jnp.where(cls == 0, x[0:128], x[128:256])
    y = jnp.where(cls == 2, x[256:384], y)
    return jnp.where(cls == 3, x[384:512], y)


def compact2(x1):
    return jnp.where(iota((32, WIDE), 1) < 4 * HEAD, x1[0:32], x1[32:64])


def stacked(x, n):
    rows = HEADS * n
    shift = n.bit_length() - 1
    own = (iota((rows, WIDE), 0) >> shift) == lane_head(rows)
    return jnp.where(own, jnp.concatenate([x] * HEADS, axis=0), 0.0).astype(BF16)


def to_tile(x, i):
    t, at, to = i // 4, 32 * (i % 4), 32 * (i // 4)
    tile = x[:, 128 * t : 128 * t + 128]
    shift = (to - at) % 128
    return pltpu.roll(tile, shift, 1) if shift else tile


def from_tiles(tiles):
    halves = []
    for t in range(2):
        lane = iota(tiles[0].shape, 1)
        half = None
        for i in range(4 * t, 4 * t + 4):
            at, to = 32 * (i % 4), 32 * (i // 4)
            shift = (at - to) % 128
            moved = pltpu.roll(tiles[i], shift, 1) if shift else tiles[i]
            half = moved if half is None else jnp.where((lane >> 5) == (i % 4), moved, half)
        halves.append(half)
    return jnp.concatenate(halves, axis=1)


def kernel(
    q_ref, k_ref, v_ref, w_ref, d_ref, len_ref,
    out_ref, dq_ref, dk_ref, dv_ref, dw_ref,
    p_s, pt_s, qt_s, kt_s, vt_s, dt_s, qx1, qx2, dx1, dx2,
    g1, g2, g3, kg23, vg23, kg1, vg1, p0s, p1s, p23s,
    a0, m0, lse_s, del_s, m1s, m23s, dqt, dkt, dvt,
    doth, att_s, po_send, po_recv,
    x1, x2, x3, y1, y2, y3, z1, z2, z3, r1, r2, r3,
    one_send, one_recv, s1, t1, s2, t2, s3, t3, u1, w1, u2, w2, u3, w3,
):
    seq = lax.axis_index("seq")
    g = lax.axis_index("head")
    chip = seq // 2
    core = seq % 2
    partner = {"seq": chip * 2 + (1 - core), "head": g}
    across = {"seq": seq, "head": 1 - g}

    def chip_at(c):
        return {"seq": c * 2 + core, "head": g}

    base1, base2 = (chip // 2) * 2, (chip // 8) * 8
    me1, me2, me3 = chip - base1, chip - base2, chip

    barrier = pltpu.get_barrier_semaphore()
    pl.semaphore_signal(barrier, inc=1, device_id=partner, device_id_type=MESH)
    pl.semaphore_signal(barrier, inc=1, device_id=across, device_id_type=MESH)

    @pl.loop(1, 32)
    def _(k):
        pl.semaphore_signal(barrier, inc=1, device_id=chip_at((chip + k) % 32), device_id_type=MESH)

    p_s[...] = (iota((ROWS, ROWS), 1) == token_of(iota((ROWS, ROWS), 0), g)).astype(F32).astype(BF16)
    pt_s[...] = (iota((ROWS, ROWS), 0) == token_of(iota((ROWS, ROWS), 1), g)).astype(F32).astype(BF16)

    def levels_of(x):
        y1_ = compact1(nn(p_s[...], x))
        y2_ = compact2(y1_)
        return y1_, y2_, y2_[0:8]

    ka, kb, kc = levels_of(k_ref[...])
    va, vb, vc = levels_of(v_ref[...])
    g1[core, me1, 0:128] = ka.astype(BF16)
    g1[core, me1, 128:256] = va.astype(BF16)
    g2[core, me2, 0:32] = kb.astype(BF16)
    g2[core, me2, 32:64] = vb.astype(BF16)
    g3[core, me3] = jnp.concatenate([kc, vc], axis=0).astype(BF16)

    pl.semaphore_wait(barrier, 33)

    def remote(src, dst, ss, rs, dev):
        return pltpu.make_async_remote_copy(
            src_ref=src, dst_ref=dst, send_sem=ss, recv_sem=rs, device_id=dev, device_id_type=MESH
        )

    send_d = remote(d_ref, doth, one_send.at[0], one_recv.at[0], across)
    send_d.start()

    def gather3(k):
        return remote(g3.at[core, me3], g3.at[core, me3], s3.at[k], t3.at[k], chip_at((chip + k) % 32))

    def gather2(k):
        return remote(
            g2.at[core, me2], g2.at[core, me2], s2.at[k], t2.at[k], chip_at(base2 + (me2 + k) % 8)
        )

    def gather1():
        return remote(g1.at[core, me1], g1.at[core, me1], s1.at[1], t1.at[1], chip_at(base1 + 1 - me1))

    gather1().start()

    @pl.loop(1, 8)
    def _(k):
        gather2(k).start()

    @pl.loop(1, 32)
    def _(k):
        gather3(k).start()

    qa, qb, _ = levels_of(q_ref[...])
    qx1[...] = stacked(qa, 128)
    qx2[...] = stacked(qb, 32)
    kt_s[...] = tn(k_ref[...], pt_s[...]).astype(BF16)
    qt_s[...] = tn(q_ref[...], pt_s[...]).astype(BF16)
    vt_s[...] = tn(v_ref[...], pt_s[...]).astype(BF16)

    start1 = len_ref[0]
    start2 = start1 + len_ref[1]
    start3 = start2 + len_ref[2]

    def ids_of(pos):
        return (
            (pos >= start1).astype(jnp.int32)
            + (pos >= start2).astype(jnp.int32)
            + (pos >= start3).astype(jnp.int32)
        )

    here = seq * ROWS
    id_k = ids_of(here + token_of(iota((ROWS, 1), 0), g))
    id_q = ids_of(here + token_of(iota((1, ROWS), 1), g))

    def head_rows(i):
        return pl.ds(pl.multiple_of(i * HEAD, 16), HEAD)

    @pl.loop(0, HEADS)
    def _(i):
        rows = head_rows(i)
        s = tn(kt_s[rows, :], qt_s[rows, :])
        s = jnp.where(id_k == id_q, s, NEG)
        top = jnp.max(s, axis=0, keepdims=True)
        p = jnp.exp2((s - top) * C2)
        total = jnp.sum(p, axis=0, keepdims=True)
        m0[pl.ds(i, 1), :] = top
        lse_s[pl.ds(i, 1), :] = top * C2 + jnp.log2(total)
        pb = p.astype(BF16)
        p0s[i] = pb
        a0[rows, :] = nn(vt_s[rows, :], pb) / total

    @pl.loop(1, 32)
    def _(k):
        gather3(k).wait()

    core3 = remote(g3.at[core], g3.at[core], s3.at[0], t3.at[0], partner)
    core3.start()

    @pl.loop(1, 8)
    def _(k):
        gather2(k).wait()

    core2 = remote(g2.at[core], g2.at[core], s2.at[0], t2.at[0], partner)
    core2.start()
    gather1().wait()
    core1 = remote(g1.at[core], g1.at[core], s1.at[0], t1.at[0], partner)
    core1.start()

    def slide_range(pos):
        lo = jnp.where(pos >= start1, start1, 0)
        lo = jnp.where(pos >= start2, start2, lo)
        lo = jnp.where(pos >= start3, start3, lo)
        hi = jnp.where(pos < start3, start3, TOKENS)
        hi = jnp.where(pos < start2, start2, hi)
        hi = jnp.where(pos < start1, start1, hi)
        return lo, hi

    def masked(s, key_pos, lo, hi):
        return jnp.where((key_pos >= lo) & (key_pos < hi), s, NEG)

    core3.wait()
    core2.wait()
    three = g3[...].astype(F32).reshape(64, 16, WIDE)
    kg23[0:512] = g2[:, :, 0:32].reshape(512, WIDE)
    vg23[0:512] = g2[:, :, 32:64].reshape(512, WIDE)
    kg23[512:1024] = three[:, 0:8].reshape(512, WIDE).astype(BF16)
    vg23[512:1024] = three[:, 8:16].reshape(512, WIDE).astype(BF16)

    row = iota((512, 1), 0)
    col = iota((1, 256), 1)
    inner = col & 31
    off = 8 * g + (col >> 5)
    lo, hi = slide_range(here + off + 16 * (inner >> 3) + 64 * (inner & 7))
    lo, hi = lo - off, hi - off
    pos2 = 512 * (2 * (base2 + ((row >> 5) & 7)) + (row >> 8)) + 16 * ((row >> 3) & 3) + 64 * (row & 7)
    pos3 = 512 * (2 * ((row >> 3) & 31) + (row >> 8)) + 64 * (row & 7)
    sa = masked(nt(kg23[0:512], qx2[...]), pos2, lo, hi)
    sb = masked(nt(kg23[512:1024], qx2[...]), pos3, jnp.where(inner < 8, lo, FAR), hi)
    top23 = jnp.maximum(jnp.max(sa, axis=0, keepdims=True), jnp.max(sb, axis=0, keepdims=True))
    pa = jnp.exp2((sa - top23) * C2)
    pb3 = jnp.exp2((sb - top23) * C2)
    sum23 = jnp.sum(pa, axis=0, keepdims=True) + jnp.sum(pb3, axis=0, keepdims=True)
    p23s[0:512] = pa.astype(BF16)
    p23s[512:1024] = pb3.astype(BF16)
    m23s[...] = jnp.broadcast_to(top23, (8, 256))
    acc23 = tn(vg23[...], p23s[...])

    core1.wait()
    kg1[...] = g1[:, :, 0:128].reshape(512, WIDE)
    vg1[...] = g1[:, :, 128:256].reshape(512, WIDE)
    colb = iota((1, 1024), 1)
    offb = (colb >> 7) & 3

    def spread1(j):
        return 4 * ((((j >> 5) & 3) + 2 * g) & 3) + 16 * ((j >> 3) & 3) + 64 * (j & 7)

    lo1, hi1 = slide_range(here + offb + spread1(colb & 127))
    lo1, hi1 = lo1 - offb, hi1 - offb
    pos1 = 512 * (2 * (base1 + ((row >> 7) & 1)) + (row >> 8)) + spread1(row & 127)
    sc = masked(nt(kg1[...], qx1[...]), pos1, lo1, hi1)
    top1 = jnp.max(sc, axis=0, keepdims=True)
    pc = jnp.exp2((sc - top1) * C2)
    sum1 = jnp.sum(pc, axis=0, keepdims=True)
    p1s[...] = pc.astype(BF16)
    m1s[...] = jnp.broadcast_to(top1, (8, 1024))
    acc1 = tn(vg1[...], p1s[...])

    st23 = jnp.broadcast_to(top23, (8, 256))
    su23 = jnp.broadcast_to(sum23, (8, 256))
    lane8 = iota((8, 128), 1) >> 5
    lane48 = iota((HEAD, 128), 1) >> 5
    for i in range(HEADS):
        r = slice(HEAD * i, HEAD * i + HEAD)
        c = slice(128 * (i % 4), 128 * (i % 4) + 128)
        t = slice(128 * i, 128 * i + 128)
        two = jnp.where(lane8 == i // 4, to_tile(st23, i), NEG)[0:1]
        two_sum = jnp.where(lane8 == i // 4, to_tile(su23, i), 0.0)[0:1]
        two_acc = jnp.where(lane48 == i // 4, to_tile(acc23[r], i), 0.0)
        zero = lse_s[i : i + 1, c]
        one = top1[:, t] * C2
        two = two * C2
        new = jnp.maximum(jnp.maximum(zero, one), two)
        f0 = jnp.exp2(zero - new)
        f1 = jnp.exp2(one - new)
        f2 = jnp.exp2(two - new)
        l_new = f0 + sum1[:, t] * f1 + two_sum * f2
        a_new = (a0[r, c] * f0 + acc1[r, t] * f1 + two_acc * f2) / l_new
        a0[r, c] = a_new
        lse_s[i : i + 1, c] = new + jnp.log2(l_new)

    att_t = a0[...].astype(BF16)
    att = nt(pt_s[...], att_t).astype(BF16)
    att_s[...] = att
    own = pl.ds(pl.multiple_of(g * WIDE, 128), WIDE)
    other = pl.ds(pl.multiple_of((1 - g) * WIDE, 128), WIDE)
    po_send[...] = nn(att, w_ref[:, other]).astype(BF16)
    send_o = remote(po_send, po_recv, one_send.at[1], one_recv.at[1], across)
    send_o.start()

    send_d.wait()
    d_att = (nt(d_ref[...], w_ref[:, own]) + nt(doth[...], w_ref[:, other])).astype(BF16)
    dt = tn(d_att, pt_s[...])
    dt_s[...] = dt.astype(BF16)
    da, db, _ = levels_of(d_att)
    dx1[...] = stacked(da, 128)
    dx2[...] = stacked(db, 32)
    prod = dt * att_t.astype(F32)
    for i in range(HEADS):
        del_s[i : i + 1, :] = jnp.sum(prod[HEAD * i : HEAD * i + HEAD], axis=0, keepdims=True)

    srow = iota((512, WIDE), 0)
    u = srow & 15
    source = 12 * (2 * ((srow >> 4) & 15) + (srow >> 8)) + u
    sel = ((iota((512, WIDE), 1) == source) & (u < 12)).astype(F32).astype(BF16)
    for part, block in ((g, d_ref), (1 - g, doth)):
        term = nn(sel, tn(block[...], att).astype(BF16)).astype(BF16).reshape(2, 16, 16, WIDE)
        x3[:, pl.ds(16 * part, 16), 16:32] = term

    def tiles_of(ref):
        return [
            jnp.broadcast_to(ref[i : i + 1, 128 * (i % 4) : 128 * (i % 4) + 128], (8, 128))
            for i in range(HEADS)
        ]

    lse_tiles, del_tiles = tiles_of(lse_s), tiles_of(del_s)
    lse23 = from_tiles(lse_tiles)[0:1]
    del23 = from_tiles(del_tiles)[0:1]
    p = p23s[...].astype(F32) * jnp.exp2(m23s[0:1] * C2 - lse23)
    ds = (p * (nt(vg23[...], dx2[...]) - del23)).astype(BF16)
    dk23 = nn(ds, qx2[...])
    dv23 = nn(p.astype(BF16), dx2[...])
    dq23 = tn(kg23[...], ds)
    x2[:, :, 0:32] = dk23[0:512].reshape(2, 8, 32, WIDE).astype(BF16)
    x2[:, :, 32:64] = dv23[0:512].reshape(2, 8, 32, WIDE).astype(BF16)
    x3[:, :, 0:16] = jnp.concatenate(
        [dk23[512:1024].reshape(2, 32, 8, WIDE), dv23[512:1024].reshape(2, 32, 8, WIDE)], axis=2
    ).astype(BF16)
    swap3 = remote(x3.at[1 - core], y3, u3.at[0], w3.at[0], partner)
    swap3.start()
    swap2 = remote(x2.at[1 - core], y2, u2.at[0], w2.at[0], partner)
    swap2.start()

    lse1 = jnp.concatenate([t[0:1] for t in lse_tiles], axis=1)
    del1 = jnp.concatenate([t[0:1] for t in del_tiles], axis=1)
    p = p1s[...].astype(F32) * jnp.exp2(m1s[0:1] * C2 - lse1)
    ds = (p * (nt(vg1[...], dx1[...]) - del1)).astype(BF16)
    dk1 = nn(ds, qx1[...])
    dv1 = nn(p.astype(BF16), dx1[...])
    dq1 = tn(kg1[...], ds)
    x1[:, :, 0:128] = dk1.reshape(2, 2, 128, WIDE).astype(BF16)
    x1[:, :, 128:256] = dv1.reshape(2, 2, 128, WIDE).astype(BF16)
    swap1 = remote(x1.at[1 - core], y1, u1.at[0], w1.at[0], partner)
    swap1.start()

    swap3.wait()
    z3[...] = (x3[core].astype(F32) + y3[...].astype(F32)).astype(BF16)
    swap2.wait()
    z2[...] = (x2[core].astype(F32) + y2[...].astype(F32)).astype(BF16)
    r3[me3] = z3[me3]
    r2[me2] = z2[me2]
    swap1.wait()
    z1[...] = (x1[core].astype(F32) + y1[...].astype(F32)).astype(BF16)
    r1[me1] = z1[me1]

    def reduce3(k):
        to = (chip + k) % 32
        return remote(z3.at[to], r3.at[me3], u3.at[k], w3.at[k], chip_at(to))

    def reduce2(k):
        to = (me2 + k) % 8
        return remote(z2.at[to], r2.at[me2], u2.at[k], w2.at[k], chip_at(base2 + to))

    def reduce1():
        return remote(z1.at[1 - me1], r1.at[me1], u1.at[1], w1.at[1], chip_at(base1 + 1 - me1))

    @pl.loop(1, 32)
    def _(k):
        reduce3(k).start()

    @pl.loop(1, 8)
    def _(k):
        reduce2(k).start()

    reduce1().start()

    a0[...] = jnp.concatenate(
        [jnp.exp2(m0[...] * C2 - lse_s[...])] * (WIDE // HEADS), axis=0
    )

    @pl.loop(0, HEADS)
    def _(i):
        rows = head_rows(i)
        p = p0s[i].astype(F32) * a0[pl.ds(i, 1), :]
        pb = p.astype(BF16)
        dp = tn(vt_s[rows, :], dt_s[rows, :])
        ds = (p * (dp - del_s[pl.ds(i, 1), :])).astype(BF16)
        dqt[rows, :] = nn(kt_s[rows, :], ds)
        dkt[rows, :] = nt(qt_s[rows, :], ds)
        dvt[rows, :] = nt(dt_s[rows, :], pb)

    for i in range(HEADS):
        r = slice(HEAD * i, HEAD * i + HEAD)
        c = slice(128 * (i % 4), 128 * (i % 4) + 128)
        t = slice(128 * i, 128 * i + 128)
        two = jnp.where(lane48 == i // 4, to_tile(dq23[r], i), 0.0)
        dqt[r, c] = dqt[r, c] + dq1[r, t] + two
    dq_ref[...] = nt(pt_s[...], (dqt[...] * SCALE).astype(BF16)).astype(BF16)

    send_o.wait()
    out_ref[...] = (nn(att_s[...], w_ref[:, own]) + po_recv[...].astype(F32)).astype(BF16)

    @pl.loop(1, 32)
    def _(k):
        reduce3(k).wait()

    @pl.loop(1, 8)
    def _(k):
        reduce2(k).wait()

    reduce1().wait()
    three = jnp.sum(r3[...].astype(F32), axis=0)
    two = jnp.sum(r2[...].astype(F32), axis=0)
    one = jnp.sum(r1[...].astype(F32), axis=0)
    dw_ref[...] = three[16:32] * (TOKENS**-0.5)
    low = iota((32, WIDE), 1) < 4 * HEAD
    cls = lane_head(128) & 3

    def whole(first, second, third, level0, scale):
        second = jnp.concatenate([second[0:8] + third, second[8:32]], axis=0)
        first = jnp.concatenate(
            [
                first[0:32] + jnp.where(low, second, 0.0),
                first[32:64] + jnp.where(low, 0.0, second),
                first[64:128],
            ],
            axis=0,
        )
        first = first * scale
        full = jnp.concatenate([jnp.where(cls == j, first, 0.0) for j in range(4)], axis=0)
        total = nn(pt_s[...], full.astype(BF16)) + nt(pt_s[...], (level0 * scale).astype(BF16))
        return total.astype(BF16)

    dk_ref[...] = whole(one[0:128], two[0:32], three[0:8], dkt[...], SCALE)
    dv_ref[...] = whole(one[128:256], two[32:64], three[8:16], dvt[...], 1.0)


def shards(queries, keys, values, w_out, d_out, slide_lengths):
    vmem = pl.BlockSpec(memory_space=pltpu.VMEM)
    shape = jax.ShapeDtypeStruct

    def v(*dims, dtype=BF16):
        return pltpu.VMEM(dims, dtype)

    def sems(n):
        return pltpu.SemaphoreType.DMA((n,))

    scratch = [
        v(512, 512), v(512, 512),
        v(WIDE, 512), v(WIDE, 512), v(WIDE, 512), v(WIDE, 512),
        v(1024, WIDE), v(256, WIDE), v(1024, WIDE), v(256, WIDE),
        v(2, 2, 256, WIDE), v(2, 8, 64, WIDE), v(2, 32, 16, WIDE),
        v(1024, WIDE), v(1024, WIDE), v(512, WIDE), v(512, WIDE),
        v(8, 512, 512), v(512, 1024), v(1024, 256),
        v(WIDE, 512, dtype=F32), v(8, 512, dtype=F32),
        v(8, 512, dtype=F32), v(8, 512, dtype=F32), v(8, 1024, dtype=F32), v(8, 256, dtype=F32),
        v(WIDE, 512, dtype=F32), v(WIDE, 512, dtype=F32), v(WIDE, 512, dtype=F32),
        v(512, WIDE), v(512, WIDE), v(512, WIDE), v(512, WIDE),
        v(2, 2, 256, WIDE), v(2, 8, 64, WIDE), v(2, 32, 32, WIDE),
        v(2, 256, WIDE), v(8, 64, WIDE), v(32, 32, WIDE),
        v(2, 256, WIDE), v(8, 64, WIDE), v(32, 32, WIDE),
        v(2, 256, WIDE), v(8, 64, WIDE), v(32, 32, WIDE),
        sems(2), sems(2),
        sems(2), sems(2), sems(8), sems(8), sems(32), sems(32),
        sems(2), sems(2), sems(8), sems(8), sems(32), sems(32),
    ]
    out, dq, dk, dv, dw = pl.pallas_call(
        kernel,
        out_shape=[shape((ROWS, WIDE), BF16)] * 4 + [shape((16, WIDE), F32)],
        in_specs=[vmem] * 5 + [pl.BlockSpec(memory_space=pltpu.SMEM)],
        out_specs=[vmem] * 5,
        scratch_shapes=scratch,
        compiler_params=pltpu.CompilerParams(
            collective_id=0, has_side_effects=True, vmem_limit_bytes=60 * 1024 * 1024
        ),
    )(queries, keys, values, w_out, d_out, slide_lengths)
    return out, dq, dk, dv, dw[:12].T


def solution(mesh):
    both = P("seq", "head")
    return jax.shard_map(
        shards,
        mesh=mesh,
        in_specs=(both, both, both, P("head", None), both, P()),
        out_specs=(both, both, both, both, P("head", "seq")),
        check_vma=False,
    )
```

profile of v0, /device:TPU:1, one launch (start us, length us, event | category | flops | bytes accessed | tf_op | source)
XLA Modules:
  0.0 67.3 jit_solution(2702611182654471915)
XLA Ops:
  0.6 60.5 %shard_map.101 = (bf16[512,384]{1,0:T(8,128)(2,1)}, bf16[512,384]{1,0:T(8,128)(2,1)}, bf16[512,384]{1,0:T(8,128)(2,1)}, bf16[512,384]{1,0:T(8,128)(2,1)}, f32[16,384]{1,0:T(8,128)}) custom-call(bf16[512,384]{1,0:T(8,128)(2,1)} %q_ref.1, bf16[512,384]{1,0:T(8,128)(2,1)} %k_ref.1, bf16[512,384]{1,0:T(8,128)(2,1)} %v_ref.1, bf16[384,768]{1,0:T(8,128)(2,1)} %w_ref.1, ...), custom_call_target="tpu_custom_call" | custom-call | tf_op jit(solution)/shard_map/pallas_call | solution.py:491
  61.1 1.3 %slice_bitcast_fusion = f32[384,12]{0,1:T(8,128)} fusion(f32[16,384]{1,0:T(8,128)} %get-tuple-element.14), kind=kLoop, calls=%fused_computation | loop fusion | bytes 36864 | tf_op jit(solution)/shard_map/transpose | solution.py:501
  62.5 0.0 copy-start.2
  62.5 1.8 %copy.15 = bf16[512,384]{1,0:T(8,128)(2,1)} copy(bf16[512,384]{1,0:T(8,128)(2,1)} %get-tuple-element.20) | data formatting | bytes 786432
  64.3 0.0 copy-done.2
  64.3 0.0 copy-start.1
  64.3 0.7 %copy.16 = bf16[512,384]{1,0:T(8,128)(2,1)} copy(bf16[512,384]{1,0:T(8,128)(2,1)S(1)} %copy-done.2) | data formatting | bytes 786432
  65.1 0.4 copy-done.1
  65.4 0.0 copy-start
  65.4 0.7 %copy.17 = bf16[512,384]{1,0:T(8,128)(2,1)} copy(bf16[512,384]{1,0:T(8,128)(2,1)S(1)} %copy-done.1) | data formatting | bytes 786432
  66.2 0.4 copy-done
  66.6 0.7 %copy.18 = bf16[512,384]{1,0:T(8,128)(2,1)} copy(bf16[512,384]{1,0:T(8,128)(2,1)S(1)} %copy-done) | data formatting | bytes 786432
Async XLA Ops:
  62.5 1.8 %copy-start.2 = (bf16[512,384]{1,0:T(8,128)(2,1)S(1)}, bf16[512,384]{1,0:T(8,128)(2,1)}, u32[]{:S(2)}) copy-start(bf16[512,384]{1,0:T(8,128)(2,1)} %get-tuple-element.21) | copy-start | bytes 1179652
  64.3 1.1 %copy-start.1 = (bf16[512,384]{1,0:T(8,128)(2,1)S(1)}, bf16[512,384]{1,0:T(8,128)(2,1)}, u32[]{:S(2)}) copy-start(bf16[512,384]{1,0:T(8,128)(2,1)} %get-tuple-element.22) | copy-start | bytes 1179652
  65.4 1.1 %copy-start = (bf16[512,384]{1,0:T(8,128)(2,1)S(1)}, bf16[512,384]{1,0:T(8,128)(2,1)}, u32[]{:S(2)}) copy-start(bf16[512,384]{1,0:T(8,128)(2,1)} %get-tuple-element.23) | copy-start | bytes 1179652
where the time goes:
time: 67.6 us; the launch traced here: 67.3 us
  Pallas kernels  60.5 us (89%)
  local copies, waits for them, and re-layouts  6.2 us (9%)
    pallas_call x1, Pallas kernels, shards(): pl.pallas_call(kernel, out_shape=[shape((ROWS, WIDE), BF16)] * 4 + [shape...  60.5 us
    unnamed x10, local copies, waits for them, and re-layouts  4.85 us

commit v1 on v0

--- a/solution.py
+++ b/solution.py
@@ -88,14 +88,15 @@
 
 
 def kernel(
-    q_ref, k_ref, v_ref, w_ref, d_ref, len_ref,
+    q_in, k_in, v_in, w_in, d_in, len_in,
     out_ref, dq_ref, dk_ref, dv_ref, dw_ref,
+    q_ref, k_ref, v_ref, w_ref, d_ref, len_ref, in_sem,
     p_s, pt_s, qt_s, kt_s, vt_s, dt_s, qx1, qx2, dx1, dx2,
     g1, g2, g3, kg23, vg23, kg1, vg1, p0s, p1s, p23s,
-    a0, m0, lse_s, del_s, m1s, m23s, dqt, dkt, dvt,
+    a0, m0, lse_s, del_s, m1s, m23s, dqt, dkt, dvt, base_k, base_v,
     doth, att_s, po_send, po_recv,
-    x1, x2, x3, y1, y2, y3, z1, z2, z3, r1, r2, r3,
-    one_send, one_recv, s1, t1, s2, t2, s3, t3, u1, w1, u2, w2, u3, w3,
+    x1, x2, x3, x4, y1, y2, y3, y4, z1, z2, z3, z4, r1, r2, r3, r4,
+    one_send, one_recv, s1, t1, s2, t2, s3, t3, u1, w1, u2, w2, u3, w3, u4, w4,
 ):
     seq = lax.axis_index("seq")
     g = lax.axis_index("head")
@@ -110,6 +111,14 @@
     base1, base2 = (chip // 2) * 2, (chip // 8) * 8
     me1, me2, me3 = chip - base1, chip - base2, chip
 
+    loads = [
+        pltpu.make_async_copy(a, b, in_sem.at[n])
+        for n, (a, b) in enumerate(
+            ((k_in, k_ref), (v_in, v_ref), (q_in, q_ref), (d_in, d_ref), (w_in, w_ref), (len_in, len_ref))
+        )
+    ]
+    for load in loads:
+        load.start()
     barrier = pltpu.get_barrier_semaphore()
     pl.semaphore_signal(barrier, inc=1, device_id=partner, device_id_type=MESH)
     pl.semaphore_signal(barrier, inc=1, device_id=across, device_id_type=MESH)
@@ -126,7 +135,9 @@
         y2_ = compact2(y1_)
         return y1_, y2_, y2_[0:8]
 
+    loads[0].wait()
     ka, kb, kc = levels_of(k_ref[...])
+    loads[1].wait()
     va, vb, vc = levels_of(v_ref[...])
     g1[core, me1, 0:128] = ka.astype(BF16)
     g1[core, me1, 128:256] = va.astype(BF16)
@@ -141,9 +152,6 @@
             src_ref=src, dst_ref=dst, send_sem=ss, recv_sem=rs, device_id=dev, device_id_type=MESH
         )
 
-    send_d = remote(d_ref, doth, one_send.at[0], one_recv.at[0], across)
-    send_d.start()
-
     def gather3(k):
         return remote(g3.at[core, me3], g3.at[core, me3], s3.at[k], t3.at[k], chip_at((chip + k) % 32))
 
@@ -155,16 +163,21 @@
     def gather1():
         return remote(g1.at[core, me1], g1.at[core, me1], s1.at[1], t1.at[1], chip_at(base1 + 1 - me1))
 
+    @pl.loop(1, 32)
+    def _(k):
+        gather3(k).start()
+
+    @pl.loop(1, 8)
+    def _(k):
+        gather2(k).start()
+
     gather1().start()
 
-    @pl.loop(1, 8)
-    def _(k):
-        gather2(k).start()
-
-    @pl.loop(1, 32)
-    def _(k):
-        gather3(k).start()
-
+    loads[3].wait()
+    send_d = remote(d_ref, doth, one_send.at[0], one_recv.at[0], across)
+    send_d.start()
+
+    loads[2].wait()
     qa, qb, _ = levels_of(q_ref[...])
     qx1[...] = stacked(qa, 128)
     qx2[...] = stacked(qb, 32)
@@ -172,6 +185,7 @@
     qt_s[...] = tn(q_ref[...], pt_s[...]).astype(BF16)
     vt_s[...] = tn(v_ref[...], pt_s[...]).astype(BF16)
 
+    loads[5].wait()
     start1 = len_ref[0]
     start2 = start1 + len_ref[1]
     start3 = start2 + len_ref[2]
@@ -220,6 +234,17 @@
     gather1().wait()
     core1 = remote(g1.at[core], g1.at[core], s1.at[0], t1.at[0], partner)
     core1.start()
+
+    loads[4].wait()
+    own = pl.ds(pl.multiple_of(g * WIDE, 128), WIDE)
+    other = pl.ds(pl.multiple_of((1 - g) * WIDE, 128), WIDE)
+    send_d.wait()
+    d_att = (nt(d_ref[...], w_ref[:, own]) + nt(doth[...], w_ref[:, other])).astype(BF16)
+    dt = tn(d_att, pt_s[...])
+    dt_s[...] = dt.astype(BF16)
+    da, db, _ = levels_of(d_att)
+    dx1[...] = stacked(da, 128)
+    dx2[...] = stacked(db, 32)
 
     def slide_range(pos):
         lo = jnp.where(pos >= start1, start1, 0)
@@ -272,13 +297,17 @@
     lo1, hi1 = slide_range(here + offb + spread1(colb & 127))
     lo1, hi1 = lo1 - offb, hi1 - offb
     pos1 = 512 * (2 * (base1 + ((row >> 7) & 1)) + (row >> 8)) + spread1(row & 127)
-    sc = masked(nt(kg1[...], qx1[...]), pos1, lo1, hi1)
-    top1 = jnp.max(sc, axis=0, keepdims=True)
-    pc = jnp.exp2((sc - top1) * C2)
-    sum1 = jnp.sum(pc, axis=0, keepdims=True)
-    p1s[...] = pc.astype(BF16)
-    m1s[...] = jnp.broadcast_to(top1, (8, 1024))
-    acc1 = tn(vg1[...], p1s[...])
+    top1, sum1, acc1 = [], [], []
+    for half in range(2):
+        c = slice(512 * half, 512 * half + 512)
+        w = slice(128 * half, 128 * half + 256)
+        sc = masked(nt(kg1[:, w], qx1[c, w]), pos1, lo1[:, c], hi1[:, c])
+        top1.append(jnp.max(sc, axis=0, keepdims=True))
+        pc = jnp.exp2((sc - top1[half]) * C2)
+        sum1.append(jnp.sum(pc, axis=0, keepdims=True))
+        p1s[:, c] = pc.astype(BF16)
+        m1s[:, c] = jnp.broadcast_to(top1[half], (8, 512))
+        acc1.append(tn(vg1[:, w], p1s[:, c]))
 
     st23 = jnp.broadcast_to(top23, (8, 256))
     su23 = jnp.broadcast_to(sum23, (8, 256))
@@ -287,49 +316,52 @@
     for i in range(HEADS):
         r = slice(HEAD * i, HEAD * i + HEAD)
         c = slice(128 * (i % 4), 128 * (i % 4) + 128)
-        t = slice(128 * i, 128 * i + 128)
+        half = i // 4
+        rr = slice(HEAD * i - 128 * half, HEAD * i - 128 * half + HEAD)
         two = jnp.where(lane8 == i // 4, to_tile(st23, i), NEG)[0:1]
         two_sum = jnp.where(lane8 == i // 4, to_tile(su23, i), 0.0)[0:1]
         two_acc = jnp.where(lane48 == i // 4, to_tile(acc23[r], i), 0.0)
         zero = lse_s[i : i + 1, c]
-        one = top1[:, t] * C2
+        one = top1[half][:, c] * C2
         two = two * C2
         new = jnp.maximum(jnp.maximum(zero, one), two)
         f0 = jnp.exp2(zero - new)
         f1 = jnp.exp2(one - new)
         f2 = jnp.exp2(two - new)
-        l_new = f0 + sum1[:, t] * f1 + two_sum * f2
-        a_new = (a0[r, c] * f0 + acc1[r, t] * f1 + two_acc * f2) / l_new
+        l_new = f0 + sum1[half][:, c] * f1 + two_sum * f2
+        a_new = (a0[r, c] * f0 + acc1[half][rr, c] * f1 + two_acc * f2) / l_new
         a0[r, c] = a_new
         lse_s[i : i + 1, c] = new + jnp.log2(l_new)
 
     att_t = a0[...].astype(BF16)
     att = nt(pt_s[...], att_t).astype(BF16)
     att_s[...] = att
-    own = pl.ds(pl.multiple_of(g * WIDE, 128), WIDE)
-    other = pl.ds(pl.multiple_of((1 - g) * WIDE, 128), WIDE)
     po_send[...] = nn(att, w_ref[:, other]).astype(BF16)
     send_o = remote(po_send, po_recv, one_send.at[1], one_recv.at[1], across)
     send_o.start()
 
-    send_d.wait()
-    d_att = (nt(d_ref[...], w_ref[:, own]) + nt(doth[...], w_ref[:, other])).astype(BF16)
-    dt = tn(d_att, pt_s[...])
-    dt_s[...] = dt.astype(BF16)
-    da, db, _ = levels_of(d_att)
-    dx1[...] = stacked(da, 128)
-    dx2[...] = stacked(db, 32)
-    prod = dt * att_t.astype(F32)
+    for part, block in ((g, d_ref), (1 - g, doth)):
+        term = tn(block[...], att)
+        for c in range(16):
+            x4[0, 16 * part + c] = term[24 * c : 24 * c + 16].astype(BF16)
+            x4[1, 16 * part + c] = term[24 * c + 8 : 24 * c + 24].astype(BF16)
+    swap4 = remote(x4.at[1 - core], y4, u4.at[0], w4.at[0], partner)
+    swap4.start()
+    prod = dt_s[...].astype(F32) * att_t.astype(F32)
     for i in range(HEADS):
         del_s[i : i + 1, :] = jnp.sum(prod[HEAD * i : HEAD * i + HEAD], axis=0, keepdims=True)
 
-    srow = iota((512, WIDE), 0)
-    u = srow & 15
-    source = 12 * (2 * ((srow >> 4) & 15) + (srow >> 8)) + u
-    sel = ((iota((512, WIDE), 1) == source) & (u < 12)).astype(F32).astype(BF16)
-    for part, block in ((g, d_ref), (1 - g, doth)):
-        term = nn(sel, tn(block[...], att).astype(BF16)).astype(BF16).reshape(2, 16, 16, WIDE)
-        x3[:, pl.ds(16 * part, 16), 16:32] = term
+    swap4.wait()
+    z4[...] = (x4[core].astype(F32) + y4[...].astype(F32)).astype(BF16)
+    r4[me3] = z4[me3]
+
+    def reduce4(k):
+        to = (chip + k) % 32
+        return remote(z4.at[to], r4.at[me3], u4.at[k], w4.at[k], chip_at(to))
+
+    @pl.loop(1, 32)
+    def _(k):
+        reduce4(k).start()
 
     def tiles_of(ref):
         return [
@@ -347,7 +379,7 @@
     dq23 = tn(kg23[...], ds)
     x2[:, :, 0:32] = dk23[0:512].reshape(2, 8, 32, WIDE).astype(BF16)
     x2[:, :, 32:64] = dv23[0:512].reshape(2, 8, 32, WIDE).astype(BF16)
-    x3[:, :, 0:16] = jnp.concatenate(
+    x3[...] = jnp.concatenate(
         [dk23[512:1024].reshape(2, 32, 8, WIDE), dv23[512:1024].reshape(2, 32, 8, WIDE)], axis=2
     ).astype(BF16)
     swap3 = remote(x3.at[1 - core], y3, u3.at[0], w3.at[0], partner)
@@ -357,11 +389,20 @@
 
     lse1 = jnp.concatenate([t[0:1] for t in lse_tiles], axis=1)
     del1 = jnp.concatenate([t[0:1] for t in del_tiles], axis=1)
-    p = p1s[...].astype(F32) * jnp.exp2(m1s[0:1] * C2 - lse1)
-    ds = (p * (nt(vg1[...], dx1[...]) - del1)).astype(BF16)
-    dk1 = nn(ds, qx1[...])
-    dv1 = nn(p.astype(BF16), dx1[...])
-    dq1 = tn(kg1[...], ds)
+    dk1, dv1, dq1 = [], [], []
+    for half in range(2):
+        c = slice(512 * half, 512 * half + 512)
+        w = slice(128 * half, 128 * half + 256)
+        p = p1s[:, c].astype(F32) * jnp.exp2(m1s[0:1, c] * C2 - lse1[:, c])
+        ds = (p * (nt(vg1[:, w], dx1[c, w]) - del1[:, c])).astype(BF16)
+        dk1.append(nn(ds, qx1[c, w]))
+        dv1.append(nn(p.astype(BF16), dx1[c, w]))
+        dq1.append(tn(kg1[:, w], ds))
+
+    def joined(a, b):
+        return jnp.concatenate([a[:, 0:128], a[:, 128:256] + b[:, 0:128], b[:, 128:256]], axis=1)
+
+    dk1, dv1 = joined(*dk1), joined(*dv1)
     x1[:, :, 0:128] = dk1.reshape(2, 2, 128, WIDE).astype(BF16)
     x1[:, :, 128:256] = dv1.reshape(2, 2, 128, WIDE).astype(BF16)
     swap1 = remote(x1.at[1 - core], y1, u1.at[0], w1.at[0], partner)
@@ -416,10 +457,14 @@
     for i in range(HEADS):
         r = slice(HEAD * i, HEAD * i + HEAD)
         c = slice(128 * (i % 4), 128 * (i % 4) + 128)
-        t = slice(128 * i, 128 * i + 128)
-        two = jnp.where(lane48 == i // 4, to_tile(dq23[r], i), 0.0)
-        dqt[r, c] = dqt[r, c] + dq1[r, t] + two
+        half = i // 4
+        rr = slice(HEAD * i - 128 * half, HEAD * i - 128 * half + HEAD)
+        two = jnp.where(lane48 == half, to_tile(dq23[r], i), 0.0)
+        dqt[r, c] = dqt[r, c] + dq1[half][rr, c] + two
     dq_ref[...] = nt(pt_s[...], (dqt[...] * SCALE).astype(BF16)).astype(BF16)
+
+    for level0, scale, kept in ((dkt, SCALE, base_k), (dvt, 1.0, base_v)):
+        kept[...] = nt(pt_s[...], (level0[...] * scale).astype(BF16))
 
     send_o.wait()
     out_ref[...] = (nn(att_s[...], w_ref[:, own]) + po_recv[...].astype(F32)).astype(BF16)
@@ -427,6 +472,7 @@
     @pl.loop(1, 32)
     def _(k):
         reduce3(k).wait()
+        reduce4(k).wait()
 
     @pl.loop(1, 8)
     def _(k):
@@ -436,11 +482,12 @@
     three = jnp.sum(r3[...].astype(F32), axis=0)
     two = jnp.sum(r2[...].astype(F32), axis=0)
     one = jnp.sum(r1[...].astype(F32), axis=0)
-    dw_ref[...] = three[16:32] * (TOKENS**-0.5)
+    four = jnp.sum(r4[...].astype(F32), axis=0) * (TOKENS**-0.5)
+    dw_ref[...] = jnp.where(core == 0, four, pltpu.roll(four, 12, 0))
     low = iota((32, WIDE), 1) < 4 * HEAD
     cls = lane_head(128) & 3
 
-    def whole(first, second, third, level0, scale):
+    def whole(first, second, third, kept, scale):
         second = jnp.concatenate([second[0:8] + third, second[8:32]], axis=0)
         first = jnp.concatenate(
             [
@@ -452,15 +499,27 @@
         )
         first = first * scale
         full = jnp.concatenate([jnp.where(cls == j, first, 0.0) for j in range(4)], axis=0)
-        total = nn(pt_s[...], full.astype(BF16)) + nt(pt_s[...], (level0 * scale).astype(BF16))
-        return total.astype(BF16)
-
-    dk_ref[...] = whole(one[0:128], two[0:32], three[0:8], dkt[...], SCALE)
-    dv_ref[...] = whole(one[128:256], two[32:64], three[8:16], dvt[...], 1.0)
+        return (nn(pt_s[...], full.astype(BF16)) + kept[...]).astype(BF16)
+
+    dk_ref[...] = whole(one[0:128], two[0:32], three[0:8], base_k, SCALE)
+    dv_ref[...] = whole(one[128:256], two[32:64], three[8:16], base_v, 1.0)
+
+
+def finish(a, b, c, d, e, out, dq, dk, dv, dw, sem):
+    moves = [
+        pltpu.make_async_copy(given, result, sem.at[n])
+        for n, (given, result) in enumerate(((a, out), (b, dq), (c, dk), (d, dv)))
+    ]
+    for move in moves:
+        move.start()
+    dw[...] = e[0:12]
+    for move in moves:
+        move.wait()
 
 
 def shards(queries, keys, values, w_out, d_out, slide_lengths):
     vmem = pl.BlockSpec(memory_space=pltpu.VMEM)
+    anywhere = pl.BlockSpec(memory_space=pl.ANY)
     shape = jax.ShapeDtypeStruct
 
     def v(*dims, dtype=BF16):
@@ -470,6 +529,8 @@
         return pltpu.SemaphoreType.DMA((n,))
 
     scratch = [
+        v(512, WIDE), v(512, WIDE), v(512, WIDE), v(WIDE, 768), v(512, WIDE),
+        pltpu.SMEM((4,), jnp.int32), sems(6),
         v(512, 512), v(512, 512),
         v(WIDE, 512), v(WIDE, 512), v(WIDE, 512), v(WIDE, 512),
         v(1024, WIDE), v(256, WIDE), v(1024, WIDE), v(256, WIDE),
@@ -479,26 +540,35 @@
         v(WIDE, 512, dtype=F32), v(8, 512, dtype=F32),
         v(8, 512, dtype=F32), v(8, 512, dtype=F32), v(8, 1024, dtype=F32), v(8, 256, dtype=F32),
         v(WIDE, 512, dtype=F32), v(WIDE, 512, dtype=F32), v(WIDE, 512, dtype=F32),
+        v(512, WIDE, dtype=F32), v(512, WIDE, dtype=F32),
         v(512, WIDE), v(512, WIDE), v(512, WIDE), v(512, WIDE),
-        v(2, 2, 256, WIDE), v(2, 8, 64, WIDE), v(2, 32, 32, WIDE),
-        v(2, 256, WIDE), v(8, 64, WIDE), v(32, 32, WIDE),
-        v(2, 256, WIDE), v(8, 64, WIDE), v(32, 32, WIDE),
-        v(2, 256, WIDE), v(8, 64, WIDE), v(32, 32, WIDE),
+        v(2, 2, 256, WIDE), v(2, 8, 64, WIDE), v(2, 32, 16, WIDE), v(2, 32, 16, WIDE),
+        v(2, 256, WIDE), v(8, 64, WIDE), v(32, 16, WIDE), v(32, 16, WIDE),
+        v(2, 256, WIDE), v(8, 64, WIDE), v(32, 16, WIDE), v(32, 16, WIDE),
+        v(2, 256, WIDE), v(8, 64, WIDE), v(32, 16, WIDE), v(32, 16, WIDE),
         sems(2), sems(2),
         sems(2), sems(2), sems(8), sems(8), sems(32), sems(32),
-        sems(2), sems(2), sems(8), sems(8), sems(32), sems(32),
+        sems(2), sems(2), sems(8), sems(8), sems(32), sems(32), sems(32), sems(32),
     ]
     out, dq, dk, dv, dw = pl.pallas_call(
         kernel,
         out_shape=[shape((ROWS, WIDE), BF16)] * 4 + [shape((16, WIDE), F32)],
-        in_specs=[vmem] * 5 + [pl.BlockSpec(memory_space=pltpu.SMEM)],
+        in_specs=[anywhere] * 6,
         out_specs=[vmem] * 5,
         scratch_shapes=scratch,
         compiler_params=pltpu.CompilerParams(
-            collective_id=0, has_side_effects=True, vmem_limit_bytes=60 * 1024 * 1024
+            collective_id=0, has_side_effects=True, vmem_limit_bytes=54_800_000
         ),
     )(queries, keys, values, w_out, d_out, slide_lengths)
-    return out, dq, dk, dv, dw[:12].T
+    out, dq, dk, dv, dw = pl.pallas_call(
+        finish,
+        out_shape=[shape((ROWS, WIDE), BF16)] * 4 + [shape((12, WIDE), F32)],
+        in_specs=[anywhere] * 4 + [vmem],
+        out_specs=[anywhere] * 4 + [vmem],
+        scratch_shapes=[sems(4)],
+        compiler_params=pltpu.CompilerParams(vmem_limit_bytes=4 * 1024 * 1024),
+    )(out, dq, dk, dv, dw)
+    return out, dq, dk, dv, dw.T
 
 
 def solution(mesh):

time: 67.6 us -> 58 us (0.86)
  local copies, waits for them, and re-layouts: 6.2 us -> 0.65 us
  Pallas kernels: 60.5 us -> 56.6 us
    pallas_call x1, Pallas kernels: 60.5 us -> 54.8 us  [shards(): pl.pallas_call(kernel, out_shape=[shape((ROWS, WIDE), BF16)] * 4 + [shape...]
    unnamed x10 -> x2, local copies, waits for them, and re-layouts: 4.85 us -> 0.65 us
    pallas_call x0 -> x1, Pallas kernels: none -> 1.78 us  [shards(): pl.pallas_call(finish, out_shape=[shape((ROWS, WIDE), BF16)] * 4 + [shape...]
    transpose x1 -> x0, local copies, waits for them, and re-layouts: 1.35 us -> none  [shards(): return (out, dq, dk, dv, dw[:12].T)]
where the time goes in v1:
time: 58 us; the launch traced here: 57.9 us
  Pallas kernels  56.6 us (98%)
  local copies, waits for them, and re-layouts  0.65 us (1%)
  between operations  0.65 us (1%)
    pallas_call x1, Pallas kernels, shards(): pl.pallas_call(kernel, out_shape=[shape((ROWS, WIDE), BF16)] * 4 + [shape...  54.8 us
    pallas_call x1, Pallas kernels, shards(): pl.pallas_call(finish, out_shape=[shape((ROWS, WIDE), BF16)] * 4 + [shape...  1.78 us

profile of v1, /device:TPU:1, one launch (start us, length us, event | category | flops | bytes accessed | tf_op | source)
XLA Modules:
  0.0 57.9 jit_solution(1186845833703065575)
XLA Ops:
  0.6 0.0 copy-start
  0.6 0.6 %copy-done = s32[4]{0:T(128)S(1)} copy-done((s32[4]{0:T(128)S(1)}, s32[4]{0:T(128)}, u32[]{:S(2)}) %copy-start) | copy-done | bytes 40
  1.3 54.8 %shard_map.101 = (bf16[512,384]{1,0:T(8,128)(2,1)S(1)}, bf16[512,384]{1,0:T(8,128)(2,1)S(1)}, bf16[512,384]{1,0:T(8,128)(2,1)S(1)}, bf16[512,384]{1,0:T(8,128)(2,1)S(1)}, f32[16,384]{1,0:T(8,128)S(1)}) custom-call(bf16[512,384]{1,0:T(8,128)(2,1)} %q_in.1, bf16[512,384]{1,0:T(8,128)(2,1)} %k_in.1, bf16[512,384]{1,0:T(8,128)(2,1)} %v_in.1, ...), custom_call_target="tpu_custom_call" | custom-call | tf_op jit(solution)/shard_map/pallas_call | solution.py:553
  56.1 1.8 %shard_map.102 = (bf16[512,384]{1,0:T(8,128)(2,1)}, bf16[512,384]{1,0:T(8,128)(2,1)}, bf16[512,384]{1,0:T(8,128)(2,1)}, bf16[512,384]{1,0:T(8,128)(2,1)}, f32[12,384]{1,0:T(8,128)}) custom-call(bf16[512,384]{1,0:T(8,128)(2,1)S(1)} %get-tuple-element.15.a, bf16[512,384]{1,0:T(8,128)(2,1)S(1)} %get-tuple-element.16.b, ...), custom_call_target="tpu_custom_call" | custom-call | tf_op jit(solution)/shard_map/pallas_call | solution.py:563
Async XLA Ops:
  0.6 0.7 %copy-start = (s32[4]{0:T(128)S(1)}, s32[4]{0:T(128)}, u32[]{:S(2)}) copy-start(s32[4]{0:T(128)} %len_in.1) | copy-start | bytes 52

commit v2 on v1

--- a/solution.py
+++ b/solution.py
@@ -95,7 +95,7 @@
     g1, g2, g3, kg23, vg23, kg1, vg1, p0s, p1s, p23s,
     a0, m0, lse_s, del_s, m1s, m23s, dqt, dkt, dvt, base_k, base_v,
     doth, att_s, po_send, po_recv,
-    x1, x2, x3, x4, y1, y2, y3, y4, z1, z2, z3, z4, r1, r2, r3, r4,
+    x1, x2, x3, x4, y1, y2, y3, y4, z1, z2, z3, z4, r1, r2, r3, r4, q3, q4, r5, r6,
     one_send, one_recv, s1, t1, s2, t2, s3, t3, u1, w1, u2, w2, u3, w3, u4, w4,
 ):
     seq = lax.axis_index("seq")
@@ -110,6 +110,14 @@
 
     base1, base2 = (chip // 2) * 2, (chip // 8) * 8
     me1, me2, me3 = chip - base1, chip - base2, chip
+    z, zrow = chip % 4, chip // 4
+    row_low = zrow + 1 - 2 * (zrow % 2)
+
+    def in_row(k):
+        return chip_at(4 * zrow + (z + k) % 4)
+
+    def other_row(k):
+        return (zrow + k) % 8
 
     loads = [
         pltpu.make_async_copy(a, b, in_sem.at[n])
@@ -123,9 +131,15 @@
     pl.semaphore_signal(barrier, inc=1, device_id=partner, device_id_type=MESH)
     pl.semaphore_signal(barrier, inc=1, device_id=across, device_id_type=MESH)
 
-    @pl.loop(1, 32)
-    def _(k):
-        pl.semaphore_signal(barrier, inc=1, device_id=chip_at((chip + k) % 32), device_id_type=MESH)
+    for k in range(1, 4):
+        pl.semaphore_signal(barrier, inc=1, device_id=in_row(k), device_id_type=MESH)
+        pl.semaphore_signal(
+            barrier, inc=1, device_id=chip_at(4 * row_low + (z + k) % 4), device_id_type=MESH
+        )
+    for k in range(1, 8):
+        pl.semaphore_signal(
+            barrier, inc=1, device_id=chip_at(4 * other_row(k) + z), device_id_type=MESH
+        )
 
     p_s[...] = (iota((ROWS, ROWS), 1) == token_of(iota((ROWS, ROWS), 0), g)).astype(F32).astype(BF16)
     pt_s[...] = (iota((ROWS, ROWS), 0) == token_of(iota((ROWS, ROWS), 1), g)).astype(F32).astype(BF16)
@@ -145,7 +159,7 @@
     g2[core, me2, 32:64] = vb.astype(BF16)
     g3[core, me3] = jnp.concatenate([kc, vc], axis=0).astype(BF16)
 
-    pl.semaphore_wait(barrier, 33)
+    pl.semaphore_wait(barrier, 15)
 
     def remote(src, dst, ss, rs, dev):
         return pltpu.make_async_remote_copy(
@@ -153,7 +167,11 @@
         )
 
     def gather3(k):
-        return remote(g3.at[core, me3], g3.at[core, me3], s3.at[k], t3.at[k], chip_at((chip + k) % 32))
+        return remote(g3.at[core, me3], g3.at[core, me3], s3.at[k], t3.at[k], in_row(k))
+
+    def gather4(k):
+        row = g3.at[core, pl.ds(4 * zrow, 4)]
+        return remote(row, row, s3.at[8 + k], t3.at[8 + k], chip_at(4 * other_row(k) + z))
 
     def gather2(k):
         return remote(
@@ -163,15 +181,20 @@
     def gather1():
         return remote(g1.at[core, me1], g1.at[core, me1], s1.at[1], t1.at[1], chip_at(base1 + 1 - me1))
 
-    @pl.loop(1, 32)
-    def _(k):
+    for k in range(1, 4):
         gather3(k).start()
+
+    gather1().start()
 
     @pl.loop(1, 8)
     def _(k):
         gather2(k).start()
 
-    gather1().start()
+
+    for k in range(1, 4):
+        gather3(k).wait()
+    for k in range(1, 8):
+        gather4(k).start()
 
     loads[3].wait()
     send_d = remote(d_ref, doth, one_send.at[0], one_recv.at[0], across)
@@ -204,8 +227,7 @@
     def head_rows(i):
         return pl.ds(pl.multiple_of(i * HEAD, 16), HEAD)
 
-    @pl.loop(0, HEADS)
-    def _(i):
+    def head_forward(i):
         rows = head_rows(i)
         s = tn(kt_s[rows, :], qt_s[rows, :])
         s = jnp.where(id_k == id_q, s, NEG)
@@ -218,33 +240,16 @@
         p0s[i] = pb
         a0[rows, :] = nn(vt_s[rows, :], pb) / total
 
-    @pl.loop(1, 32)
-    def _(k):
-        gather3(k).wait()
-
-    core3 = remote(g3.at[core], g3.at[core], s3.at[0], t3.at[0], partner)
-    core3.start()
-
-    @pl.loop(1, 8)
-    def _(k):
-        gather2(k).wait()
-
-    core2 = remote(g2.at[core], g2.at[core], s2.at[0], t2.at[0], partner)
-    core2.start()
+    pl.loop(0, 4, unroll=2)(head_forward)
+
     gather1().wait()
     core1 = remote(g1.at[core], g1.at[core], s1.at[0], t1.at[0], partner)
     core1.start()
-
-    loads[4].wait()
-    own = pl.ds(pl.multiple_of(g * WIDE, 128), WIDE)
-    other = pl.ds(pl.multiple_of((1 - g) * WIDE, 128), WIDE)
-    send_d.wait()
-    d_att = (nt(d_ref[...], w_ref[:, own]) + nt(doth[...], w_ref[:, other])).astype(BF16)
-    dt = tn(d_att, pt_s[...])
-    dt_s[...] = dt.astype(BF16)
-    da, db, _ = levels_of(d_att)
-    dx1[...] = stacked(da, 128)
-    dx2[...] = stacked(db, 32)
+    pl.loop(4, HEADS, unroll=2)(head_forward)
+    for k in range(1, 8):
+        gather4(k).wait()
+    core3 = remote(g3.at[core], g3.at[core], s3.at[0], t3.at[0], partner)
+    core3.start()
 
     def slide_range(pos):
         lo = jnp.where(pos >= start1, start1, 0)
@@ -258,6 +263,38 @@
     def masked(s, key_pos, lo, hi):
         return jnp.where((key_pos >= lo) & (key_pos < hi), s, NEG)
 
+    core1.wait()
+    row = iota((512, 1), 0)
+    kg1[...] = g1[:, :, 0:128].reshape(512, WIDE)
+    vg1[...] = g1[:, :, 128:256].reshape(512, WIDE)
+    colb = iota((1, 1024), 1)
+    offb = (colb >> 7) & 3
+
+    def spread1(j):
+        return 4 * ((((j >> 5) & 3) + 2 * g) & 3) + 16 * ((j >> 3) & 3) + 64 * (j & 7)
+
+    lo1, hi1 = slide_range(here + offb + spread1(colb & 127))
+    lo1, hi1 = lo1 - offb, hi1 - offb
+    pos1 = 512 * (2 * (base1 + ((row >> 7) & 1)) + (row >> 8)) + spread1(row & 127)
+    top1, sum1, acc1 = [], [], []
+    for half in range(2):
+        c = slice(512 * half, 512 * half + 512)
+        w = slice(128 * half, 128 * half + 256)
+        sc = masked(nt(kg1[:, w], qx1[c, w]), pos1, lo1[:, c], hi1[:, c])
+        top1.append(jnp.max(sc, axis=0, keepdims=True))
+        pc = jnp.exp2((sc - top1[half]) * C2)
+        sum1.append(jnp.sum(pc, axis=0, keepdims=True))
+        p1s[:, c] = pc.astype(BF16)
+        m1s[:, c] = jnp.broadcast_to(top1[half], (8, 512))
+        acc1.append(tn(vg1[:, w], p1s[:, c]))
+
+    @pl.loop(1, 8)
+    def _(k):
+        gather2(k).wait()
+
+    core2 = remote(g2.at[core], g2.at[core], s2.at[0], t2.at[0], partner)
+    core2.start()
+
     core3.wait()
     core2.wait()
     three = g3[...].astype(F32).reshape(64, 16, WIDE)
@@ -266,7 +303,6 @@
     kg23[512:1024] = three[:, 0:8].reshape(512, WIDE).astype(BF16)
     vg23[512:1024] = three[:, 8:16].reshape(512, WIDE).astype(BF16)
 
-    row = iota((512, 1), 0)
     col = iota((1, 256), 1)
     inner = col & 31
     off = 8 * g + (col >> 5)
@@ -284,30 +320,6 @@
     p23s[512:1024] = pb3.astype(BF16)
     m23s[...] = jnp.broadcast_to(top23, (8, 256))
     acc23 = tn(vg23[...], p23s[...])
-
-    core1.wait()
-    kg1[...] = g1[:, :, 0:128].reshape(512, WIDE)
-    vg1[...] = g1[:, :, 128:256].reshape(512, WIDE)
-    colb = iota((1, 1024), 1)
-    offb = (colb >> 7) & 3
-
-    def spread1(j):
-        return 4 * ((((j >> 5) & 3) + 2 * g) & 3) + 16 * ((j >> 3) & 3) + 64 * (j & 7)
-
-    lo1, hi1 = slide_range(here + offb + spread1(colb & 127))
-    lo1, hi1 = lo1 - offb, hi1 - offb
-    pos1 = 512 * (2 * (base1 + ((row >> 7) & 1)) + (row >> 8)) + spread1(row & 127)
-    top1, sum1, acc1 = [], [], []
-    for half in range(2):
-        c = slice(512 * half, 512 * half + 512)
-        w = slice(128 * half, 128 * half + 256)
-        sc = masked(nt(kg1[:, w], qx1[c, w]), pos1, lo1[:, c], hi1[:, c])
-        top1.append(jnp.max(sc, axis=0, keepdims=True))
-        pc = jnp.exp2((sc - top1[half]) * C2)
-        sum1.append(jnp.sum(pc, axis=0, keepdims=True))
-        p1s[:, c] = pc.astype(BF16)
-        m1s[:, c] = jnp.broadcast_to(top1[half], (8, 512))
-        acc1.append(tn(vg1[:, w], p1s[:, c]))
 
     st23 = jnp.broadcast_to(top23, (8, 256))
     su23 = jnp.broadcast_to(sum23, (8, 256))
@@ -336,32 +348,36 @@
     att_t = a0[...].astype(BF16)
     att = nt(pt_s[...], att_t).astype(BF16)
     att_s[...] = att
+    loads[4].wait()
+    own = pl.ds(pl.multiple_of(g * WIDE, 128), WIDE)
+    other = pl.ds(pl.multiple_of((1 - g) * WIDE, 128), WIDE)
     po_send[...] = nn(att, w_ref[:, other]).astype(BF16)
-    send_o = remote(po_send, po_recv, one_send.at[1], one_recv.at[1], across)
-    send_o.start()
-
+
+    def send_o(part):
+        rows = pl.ds(256 * part, 256)
+        n = 1 + part
+        return remote(po_send.at[rows], po_recv.at[rows], one_send.at[n], one_recv.at[n], across)
+
+    send_o(0).start()
+
+    send_d.wait()
     for part, block in ((g, d_ref), (1 - g, doth)):
         term = tn(block[...], att)
         for c in range(16):
-            x4[0, 16 * part + c] = term[24 * c : 24 * c + 16].astype(BF16)
-            x4[1, 16 * part + c] = term[24 * c + 8 : 24 * c + 24].astype(BF16)
+            x4[0, c % 4, 4 * part + c // 4] = term[24 * c : 24 * c + 16].astype(BF16)
+            x4[1, c % 4, 4 * part + c // 4] = term[24 * c + 8 : 24 * c + 24].astype(BF16)
     swap4 = remote(x4.at[1 - core], y4, u4.at[0], w4.at[0], partner)
     swap4.start()
+    d_att = (nt(d_ref[...], w_ref[:, own]) + nt(doth[...], w_ref[:, other])).astype(BF16)
+    dt = tn(d_att, pt_s[...])
+    dt_s[...] = dt.astype(BF16)
+    da, db, _ = levels_of(d_att)
+    dx1[...] = stacked(da, 128)
+    dx2[...] = stacked(db, 32)
+
     prod = dt_s[...].astype(F32) * att_t.astype(F32)
     for i in range(HEADS):
         del_s[i : i + 1, :] = jnp.sum(prod[HEAD * i : HEAD * i + HEAD], axis=0, keepdims=True)
-
-    swap4.wait()
-    z4[...] = (x4[core].astype(F32) + y4[...].astype(F32)).astype(BF16)
-    r4[me3] = z4[me3]
-
-    def reduce4(k):
-        to = (chip + k) % 32
-        return remote(z4.at[to], r4.at[me3], u4.at[k], w4.at[k], chip_at(to))
-
-    @pl.loop(1, 32)
-    def _(k):
-        reduce4(k).start()
 
     def tiles_of(ref):
         return [
@@ -387,6 +403,20 @@
     swap2 = remote(x2.at[1 - core], y2, u2.at[0], w2.at[0], partner)
     swap2.start()
 
+    swap4.wait()
+    z4[...] = (x4[core].astype(F32) + y4[...].astype(F32)).astype(BF16)
+    r4[z] = z4[z]
+
+    def reduce4(k):
+        return remote(z4.at[(z + k) % 4], r4.at[z], u4.at[k], w4.at[k], in_row(k))
+
+    def reduce6(k):
+        to = other_row(k)
+        return remote(q4.at[to], r6.at[zrow], u4.at[8 + k], w4.at[8 + k], chip_at(4 * to + z))
+
+    for k in range(1, 4):
+        reduce4(k).start()
+
     lse1 = jnp.concatenate([t[0:1] for t in lse_tiles], axis=1)
     del1 = jnp.concatenate([t[0:1] for t in del_tiles], axis=1)
     dk1, dv1, dq1 = [], [], []
@@ -412,15 +442,16 @@
     z3[...] = (x3[core].astype(F32) + y3[...].astype(F32)).astype(BF16)
     swap2.wait()
     z2[...] = (x2[core].astype(F32) + y2[...].astype(F32)).astype(BF16)
-    r3[me3] = z3[me3]
+    r3[zrow] = z3[pl.ds(4 * zrow, 4)]
     r2[me2] = z2[me2]
-    swap1.wait()
-    z1[...] = (x1[core].astype(F32) + y1[...].astype(F32)).astype(BF16)
-    r1[me1] = z1[me1]
-
     def reduce3(k):
-        to = (chip + k) % 32
-        return remote(z3.at[to], r3.at[me3], u3.at[k], w3.at[k], chip_at(to))
+        to = other_row(k)
+        return remote(
+            z3.at[pl.ds(4 * to, 4)], r3.at[zrow], u3.at[k], w3.at[k], chip_at(4 * to + z)
+        )
+
+    def reduce5(k):
+        return remote(q3.at[(z + k) % 4], r5.at[z], u3.at[8 + k], w3.at[8 + k], in_row(k))
 
     def reduce2(k):
         to = (me2 + k) % 8
@@ -429,22 +460,20 @@
     def reduce1():
         return remote(z1.at[1 - me1], r1.at[me1], u1.at[1], w1.at[1], chip_at(base1 + 1 - me1))
 
-    @pl.loop(1, 32)
-    def _(k):
+    for k in range(1, 8):
         reduce3(k).start()
 
     @pl.loop(1, 8)
     def _(k):
         reduce2(k).start()
 
-    reduce1().start()
+    send_o(1).start()
 
     a0[...] = jnp.concatenate(
         [jnp.exp2(m0[...] * C2 - lse_s[...])] * (WIDE // HEADS), axis=0
     )
 
-    @pl.loop(0, HEADS)
-    def _(i):
+    def head_back(i):
         rows = head_rows(i)
         p = p0s[i].astype(F32) * a0[pl.ds(i, 1), :]
         pb = p.astype(BF16)
@@ -454,6 +483,26 @@
         dkt[rows, :] = nt(qt_s[rows, :], ds)
         dvt[rows, :] = nt(dt_s[rows, :], pb)
 
+    pl.loop(0, 2, unroll=2)(head_back)
+    swap1.wait()
+    z1[...] = (x1[core].astype(F32) + y1[...].astype(F32)).astype(BF16)
+    r1[me1] = z1[me1]
+    reduce1().start()
+    for k in range(1, 4):
+        reduce4(k).wait()
+    q4[...] = jnp.sum(r4[...].astype(F32), axis=0).astype(BF16)
+    r6[zrow] = q4[zrow]
+    for k in range(1, 8):
+        reduce6(k).start()
+    pl.loop(2, 6, unroll=2)(head_back)
+    for k in range(1, 8):
+        reduce3(k).wait()
+    q3[...] = jnp.sum(r3[...].astype(F32), axis=0).astype(BF16)
+    r5[z] = q3[z]
+    for k in range(1, 4):
+        reduce5(k).start()
+    pl.loop(6, 8, unroll=2)(head_back)
+
     for i in range(HEADS):
         r = slice(HEAD * i, HEAD * i + HEAD)
         c = slice(128 * (i % 4), 128 * (i % 4) + 128)
@@ -466,23 +515,24 @@
     for level0, scale, kept in ((dkt, SCALE, base_k), (dvt, 1.0, base_v)):
         kept[...] = nt(pt_s[...], (level0[...] * scale).astype(BF16))
 
-    send_o.wait()
+    send_o(0).wait()
+    send_o(1).wait()
     out_ref[...] = (nn(att_s[...], w_ref[:, own]) + po_recv[...].astype(F32)).astype(BF16)
 
-    @pl.loop(1, 32)
-    def _(k):
-        reduce3(k).wait()
-        reduce4(k).wait()
+    for k in range(1, 8):
+        reduce6(k).wait()
+    for k in range(1, 4):
+        reduce5(k).wait()
 
     @pl.loop(1, 8)
     def _(k):
         reduce2(k).wait()
 
     reduce1().wait()
-    three = jnp.sum(r3[...].astype(F32), axis=0)
+    three = jnp.sum(r5[...].astype(F32), axis=0)
     two = jnp.sum(r2[...].astype(F32), axis=0)
     one = jnp.sum(r1[...].astype(F32), axis=0)
-    four = jnp.sum(r4[...].astype(F32), axis=0) * (TOKENS**-0.5)
+    four = jnp.sum(r6[...].astype(F32), axis=0) * (TOKENS**-0.5)
     dw_ref[...] = jnp.where(core == 0, four, pltpu.roll(four, 12, 0))
     low = iota((32, WIDE), 1) < 4 * HEAD
     cls = lane_head(128) & 3
@@ -542,11 +592,12 @@
         v(WIDE, 512, dtype=F32), v(WIDE, 512, dtype=F32), v(WIDE, 512, dtype=F32),
         v(512, WIDE, dtype=F32), v(512, WIDE, dtype=F32),
         v(512, WIDE), v(512, WIDE), v(512, WIDE), v(512, WIDE),
-        v(2, 2, 256, WIDE), v(2, 8, 64, WIDE), v(2, 32, 16, WIDE), v(2, 32, 16, WIDE),
-        v(2, 256, WIDE), v(8, 64, WIDE), v(32, 16, WIDE), v(32, 16, WIDE),
-        v(2, 256, WIDE), v(8, 64, WIDE), v(32, 16, WIDE), v(32, 16, WIDE),
-        v(2, 256, WIDE), v(8, 64, WIDE), v(32, 16, WIDE), v(32, 16, WIDE),
-        sems(2), sems(2),
+        v(2, 2, 256, WIDE), v(2, 8, 64, WIDE), v(2, 32, 16, WIDE), v(2, 4, 8, 16, WIDE),
+        v(2, 256, WIDE), v(8, 64, WIDE), v(32, 16, WIDE), v(4, 8, 16, WIDE),
+        v(2, 256, WIDE), v(8, 64, WIDE), v(32, 16, WIDE), v(4, 8, 16, WIDE),
+        v(2, 256, WIDE), v(8, 64, WIDE), v(8, 4, 16, WIDE), v(4, 8, 16, WIDE),
+        v(4, 16, WIDE), v(8, 16, WIDE), v(4, 16, WIDE), v(8, 16, WIDE),
+        sems(3), sems(3),
         sems(2), sems(2), sems(8), sems(8), sems(32), sems(32),
         sems(2), sems(2), sems(8), sems(8), sems(32), sems(32), sems(32), sems(32),
     ]

time: 58 us -> 50.9 us (0.88)
  Pallas kernels: 56.6 us -> 49.3 us
    pallas_call x1, Pallas kernels: 54.8 us -> 47.5 us  [shards(): pl.pallas_call(kernel, out_shape=[shape((ROWS, WIDE), BF16)] * 4 + [shape...]
where the time goes in v2:
time: 50.9 us; the launch traced here: 50.8 us
  Pallas kernels  49.3 us (97%)
  between operations  0.81 us (2%)
  local copies, waits for them, and re-layouts  0.65 us (1%)
    pallas_call x1, Pallas kernels, shards(): pl.pallas_call(kernel, out_shape=[shape((ROWS, WIDE), BF16)] * 4 + [shape...  47.5 us
    pallas_call x1, Pallas kernels, shards(): pl.pallas_call(finish, out_shape=[shape((ROWS, WIDE), BF16)] * 4 + [shape...  1.78 us

profile of v2, /device:TPU:1, one launch (start us, length us, event | category | flops | bytes accessed | tf_op | source)
XLA Modules:
  0.0 50.8 jit_solution(7962673561518549183)
XLA Ops:
  0.6 0.0 copy-start
  0.6 0.6 %copy-done = s32[4]{0:T(128)S(1)} copy-done((s32[4]{0:T(128)S(1)}, s32[4]{0:T(128)}, u32[]{:S(2)}) %copy-start) | copy-done | bytes 40
  1.3 47.5 %shard_map.101 = (bf16[512,384]{1,0:T(8,128)(2,1)S(1)}, bf16[512,384]{1,0:T(8,128)(2,1)S(1)}, bf16[512,384]{1,0:T(8,128)(2,1)S(1)}, bf16[512,384]{1,0:T(8,128)(2,1)S(1)}, f32[16,384]{1,0:T(8,128)S(1)}) custom-call(bf16[512,384]{1,0:T(8,128)(2,1)} %q_in.1, bf16[512,384]{1,0:T(8,128)(2,1)} %k_in.1, bf16[512,384]{1,0:T(8,128)(2,1)} %v_in.1, ...), custom_call_target="tpu_custom_call" | custom-call | tf_op jit(solution)/shard_map/pallas_call | solution.py:604
  48.8 1.8 %shard_map.102 = (bf16[512,384]{1,0:T(8,128)(2,1)}, bf16[512,384]{1,0:T(8,128)(2,1)}, bf16[512,384]{1,0:T(8,128)(2,1)}, bf16[512,384]{1,0:T(8,128)(2,1)}, f32[12,384]{1,0:T(8,128)}) custom-call(bf16[512,384]{1,0:T(8,128)(2,1)S(1)} %get-tuple-element.15.a, bf16[512,384]{1,0:T(8,128)(2,1)S(1)} %get-tuple-element.16.b, ...), custom_call_target="tpu_custom_call" | custom-call | tf_op jit(solution)/shard_map/pallas_call | solution.py:614
Async XLA Ops:
  0.6 0.7 %copy-start = (s32[4]{0:T(128)S(1)}, s32[4]{0:T(128)}, u32[]{:S(2)}) copy-start(s32[4]{0:T(128)} %len_in.1) | copy-start | bytes 52

commit v3 on v2

--- a/solution.py
+++ b/solution.py
@@ -125,8 +125,8 @@
             ((k_in, k_ref), (v_in, v_ref), (q_in, q_ref), (d_in, d_ref), (w_in, w_ref), (len_in, len_ref))
         )
     ]
-    for load in loads:
-        load.start()
+    loads[0].start()
+    loads[1].start()
     barrier = pltpu.get_barrier_semaphore()
     pl.semaphore_signal(barrier, inc=1, device_id=partner, device_id_type=MESH)
     pl.semaphore_signal(barrier, inc=1, device_id=across, device_id_type=MESH)
@@ -142,7 +142,6 @@
         )
 
     p_s[...] = (iota((ROWS, ROWS), 1) == token_of(iota((ROWS, ROWS), 0), g)).astype(F32).astype(BF16)
-    pt_s[...] = (iota((ROWS, ROWS), 0) == token_of(iota((ROWS, ROWS), 1), g)).astype(F32).astype(BF16)
 
     def levels_of(x):
         y1_ = compact1(nn(p_s[...], x))
@@ -152,6 +151,8 @@
     loads[0].wait()
     ka, kb, kc = levels_of(k_ref[...])
     loads[1].wait()
+    for n in (2, 3, 4, 5):
+        loads[n].start()
     va, vb, vc = levels_of(v_ref[...])
     g1[core, me1, 0:128] = ka.astype(BF16)
     g1[core, me1, 128:256] = va.astype(BF16)
@@ -201,6 +202,7 @@
     send_d.start()
 
     loads[2].wait()
+    pt_s[...] = (iota((ROWS, ROWS), 0) == token_of(iota((ROWS, ROWS), 1), g)).astype(F32).astype(BF16)
     qa, qb, _ = levels_of(q_ref[...])
     qx1[...] = stacked(qa, 128)
     qx2[...] = stacked(qb, 32)
@@ -241,6 +243,11 @@
         a0[rows, :] = nn(vt_s[rows, :], pb) / total
 
     pl.loop(0, 4, unroll=2)(head_forward)
+
+    loads[4].wait()
+    own = pl.ds(pl.multiple_of(g * WIDE, 128), WIDE)
+    other = pl.ds(pl.multiple_of((1 - g) * WIDE, 128), WIDE)
+    base_k[...] = nt(d_ref[...], w_ref[:, own])
 
     gather1().wait()
     core1 = remote(g1.at[core], g1.at[core], s1.at[0], t1.at[0], partner)
@@ -348,9 +355,6 @@
     att_t = a0[...].astype(BF16)
     att = nt(pt_s[...], att_t).astype(BF16)
     att_s[...] = att
-    loads[4].wait()
-    own = pl.ds(pl.multiple_of(g * WIDE, 128), WIDE)
-    other = pl.ds(pl.multiple_of((1 - g) * WIDE, 128), WIDE)
     po_send[...] = nn(att, w_ref[:, other]).astype(BF16)
 
     def send_o(part):
@@ -359,6 +363,7 @@
         return remote(po_send.at[rows], po_recv.at[rows], one_send.at[n], one_recv.at[n], across)
 
     send_o(0).start()
+    send_o(1).start()
 
     send_d.wait()
     for part, block in ((g, d_ref), (1 - g, doth)):
@@ -368,7 +373,7 @@
             x4[1, c % 4, 4 * part + c // 4] = term[24 * c + 8 : 24 * c + 24].astype(BF16)
     swap4 = remote(x4.at[1 - core], y4, u4.at[0], w4.at[0], partner)
     swap4.start()
-    d_att = (nt(d_ref[...], w_ref[:, own]) + nt(doth[...], w_ref[:, other])).astype(BF16)
+    d_att = (base_k[...] + nt(doth[...], w_ref[:, other])).astype(BF16)
     dt = tn(d_att, pt_s[...])
     dt_s[...] = dt.astype(BF16)
     da, db, _ = levels_of(d_att)
@@ -378,6 +383,20 @@
     prod = dt_s[...].astype(F32) * att_t.astype(F32)
     for i in range(HEADS):
         del_s[i : i + 1, :] = jnp.sum(prod[HEAD * i : HEAD * i + HEAD], axis=0, keepdims=True)
+
+    swap4.wait()
+    z4[...] = (x4[core].astype(F32) + y4[...].astype(F32)).astype(BF16)
+    r4[z] = z4[z]
+
+    def reduce4(k):
+        return remote(z4.at[(z + k) % 4], r4.at[z], u4.at[k], w4.at[k], in_row(k))
+
+    def reduce6(k):
+        to = other_row(k)
+        return remote(q4.at[to], r6.at[zrow], u4.at[8 + k], w4.at[8 + k], chip_at(4 * to + z))
+
+    for k in range(1, 4):
+        reduce4(k).start()
 
     def tiles_of(ref):
         return [
@@ -403,24 +422,35 @@
     swap2 = remote(x2.at[1 - core], y2, u2.at[0], w2.at[0], partner)
     swap2.start()
 
-    swap4.wait()
-    z4[...] = (x4[core].astype(F32) + y4[...].astype(F32)).astype(BF16)
-    r4[z] = z4[z]
-
-    def reduce4(k):
-        return remote(z4.at[(z + k) % 4], r4.at[z], u4.at[k], w4.at[k], in_row(k))
-
-    def reduce6(k):
-        to = other_row(k)
-        return remote(q4.at[to], r6.at[zrow], u4.at[8 + k], w4.at[8 + k], chip_at(4 * to + z))
-
-    for k in range(1, 4):
-        reduce4(k).start()
-
     lse1 = jnp.concatenate([t[0:1] for t in lse_tiles], axis=1)
     del1 = jnp.concatenate([t[0:1] for t in del_tiles], axis=1)
+    def reduce3(k):
+        to = other_row(k)
+        return remote(
+            z3.at[pl.ds(4 * to, 4)], r3.at[zrow], u3.at[k], w3.at[k], chip_at(4 * to + z)
+        )
+
+    def reduce5(k):
+        return remote(q3.at[(z + k) % 4], r5.at[z], u3.at[8 + k], w3.at[8 + k], in_row(k))
+
+    def reduce2(k):
+        to = (me2 + k) % 8
+        return remote(z2.at[to], r2.at[me2], u2.at[k], w2.at[k], chip_at(base2 + to))
+
+    def reduce1():
+        return remote(z1.at[1 - me1], r1.at[me1], u1.at[1], w1.at[1], chip_at(base1 + 1 - me1))
+
+    def send_third():
+        swap3.wait()
+        z3[...] = (x3[core].astype(F32) + y3[...].astype(F32)).astype(BF16)
+        r3[zrow] = z3[pl.ds(4 * zrow, 4)]
+        for k in range(1, 8):
+            reduce3(k).start()
+
     dk1, dv1, dq1 = [], [], []
     for half in range(2):
+        if half == 1:
+            send_third()
         c = slice(512 * half, 512 * half + 512)
         w = slice(128 * half, 128 * half + 256)
         p = p1s[:, c].astype(F32) * jnp.exp2(m1s[0:1, c] * C2 - lse1[:, c])
@@ -438,36 +468,13 @@
     swap1 = remote(x1.at[1 - core], y1, u1.at[0], w1.at[0], partner)
     swap1.start()
 
-    swap3.wait()
-    z3[...] = (x3[core].astype(F32) + y3[...].astype(F32)).astype(BF16)
     swap2.wait()
     z2[...] = (x2[core].astype(F32) + y2[...].astype(F32)).astype(BF16)
-    r3[zrow] = z3[pl.ds(4 * zrow, 4)]
     r2[me2] = z2[me2]
-    def reduce3(k):
-        to = other_row(k)
-        return remote(
-            z3.at[pl.ds(4 * to, 4)], r3.at[zrow], u3.at[k], w3.at[k], chip_at(4 * to + z)
-        )
-
-    def reduce5(k):
-        return remote(q3.at[(z + k) % 4], r5.at[z], u3.at[8 + k], w3.at[8 + k], in_row(k))
-
-    def reduce2(k):
-        to = (me2 + k) % 8
-        return remote(z2.at[to], r2.at[me2], u2.at[k], w2.at[k], chip_at(base2 + to))
-
-    def reduce1():
-        return remote(z1.at[1 - me1], r1.at[me1], u1.at[1], w1.at[1], chip_at(base1 + 1 - me1))
-
-    for k in range(1, 8):
-        reduce3(k).start()
 
     @pl.loop(1, 8)
     def _(k):
         reduce2(k).start()
-
-    send_o(1).start()
 
     a0[...] = jnp.concatenate(
         [jnp.exp2(m0[...] * C2 - lse_s[...])] * (WIDE // HEADS), axis=0
@@ -494,14 +501,14 @@
     r6[zrow] = q4[zrow]
     for k in range(1, 8):
         reduce6(k).start()
-    pl.loop(2, 6, unroll=2)(head_back)
+    pl.loop(2, 4, unroll=2)(head_back)
     for k in range(1, 8):
         reduce3(k).wait()
     q3[...] = jnp.sum(r3[...].astype(F32), axis=0).astype(BF16)
     r5[z] = q3[z]
     for k in range(1, 4):
         reduce5(k).start()
-    pl.loop(6, 8, unroll=2)(head_back)
+    pl.loop(4, 8, unroll=4)(head_back)
 
     for i in range(HEADS):
         r = slice(HEAD * i, HEAD * i + HEAD)
@@ -515,25 +522,24 @@
     for level0, scale, kept in ((dkt, SCALE, base_k), (dvt, 1.0, base_v)):
         kept[...] = nt(pt_s[...], (level0[...] * scale).astype(BF16))
 
+    for k in range(1, 8):
+        reduce6(k).wait()
+    four = jnp.sum(r6[...].astype(F32), axis=0) * (TOKENS**-0.5)
+    dw_ref[...] = jnp.where(core == 0, four, pltpu.roll(four, 12, 0))
+
+    @pl.loop(1, 8)
+    def _(k):
+        reduce2(k).wait()
+
+    two = jnp.sum(r2[...].astype(F32), axis=0)
     send_o(0).wait()
     send_o(1).wait()
     out_ref[...] = (nn(att_s[...], w_ref[:, own]) + po_recv[...].astype(F32)).astype(BF16)
-
-    for k in range(1, 8):
-        reduce6(k).wait()
     for k in range(1, 4):
         reduce5(k).wait()
-
-    @pl.loop(1, 8)
-    def _(k):
-        reduce2(k).wait()
-
+    three = jnp.sum(r5[...].astype(F32), axis=0)
     reduce1().wait()
-    three = jnp.sum(r5[...].astype(F32), axis=0)
-    two = jnp.sum(r2[...].astype(F32), axis=0)
     one = jnp.sum(r1[...].astype(F32), axis=0)
-    four = jnp.sum(r6[...].astype(F32), axis=0) * (TOKENS**-0.5)
-    dw_ref[...] = jnp.where(core == 0, four, pltpu.roll(four, 12, 0))
     low = iota((32, WIDE), 1) < 4 * HEAD
     cls = lane_head(128) & 3
 

time: 50.9 us -> 50 us (0.982)
  Pallas kernels: 49.3 us -> 48.4 us
    pallas_call x1, Pallas kernels: 47.5 us -> 46.7 us  [shards(): pl.pallas_call(kernel, out_shape=[shape((ROWS, WIDE), BF16)] * 4 + [shape...]
where the time goes in v3:
time: 50 us; the launch traced here: 49.9 us
  Pallas kernels  48.4 us (97%)
  between operations  0.81 us (2%)
  local copies, waits for them, and re-layouts  0.65 us (1%)
    pallas_call x1, Pallas kernels, shards(): pl.pallas_call(kernel, out_shape=[shape((ROWS, WIDE), BF16)] * 4 + [shape...  46.7 us
    pallas_call x1, Pallas kernels, shards(): pl.pallas_call(finish, out_shape=[shape((ROWS, WIDE), BF16)] * 4 + [shape...  1.78 us

profile of v3, /device:TPU:1, one launch (start us, length us, event | category | flops | bytes accessed | tf_op | source)
XLA Modules:
  0.0 49.9 jit_solution(9563797256432497421)
XLA Ops:
  0.6 0.0 copy-start
  0.6 0.6 %copy-done = s32[4]{0:T(128)S(1)} copy-done((s32[4]{0:T(128)S(1)}, s32[4]{0:T(128)}, u32[]{:S(2)}) %copy-start) | copy-done | bytes 40
  1.3 46.7 %shard_map.101 = (bf16[512,384]{1,0:T(8,128)(2,1)S(1)}, bf16[512,384]{1,0:T(8,128)(2,1)S(1)}, bf16[512,384]{1,0:T(8,128)(2,1)S(1)}, bf16[512,384]{1,0:T(8,128)(2,1)S(1)}, f32[16,384]{1,0:T(8,128)S(1)}) custom-call(bf16[512,384]{1,0:T(8,128)(2,1)} %q_in.1, bf16[512,384]{1,0:T(8,128)(2,1)} %k_in.1, bf16[512,384]{1,0:T(8,128)(2,1)} %v_in.1, ...), custom_call_target="tpu_custom_call" | custom-call | tf_op jit(solution)/shard_map/pallas_call | solution.py:610
  48.0 1.8 %shard_map.102 = (bf16[512,384]{1,0:T(8,128)(2,1)}, bf16[512,384]{1,0:T(8,128)(2,1)}, bf16[512,384]{1,0:T(8,128)(2,1)}, bf16[512,384]{1,0:T(8,128)(2,1)}, f32[12,384]{1,0:T(8,128)}) custom-call(bf16[512,384]{1,0:T(8,128)(2,1)S(1)} %get-tuple-element.15.a, bf16[512,384]{1,0:T(8,128)(2,1)S(1)} %get-tuple-element.16.b, ...), custom_call_target="tpu_custom_call" | custom-call | tf_op jit(solution)/shard_map/pallas_call | solution.py:620
Async XLA Ops:
  0.6 0.7 %copy-start = (s32[4]{0:T(128)S(1)}, s32[4]{0:T(128)}, u32[]{:S(2)}) copy-start(s32[4]{0:T(128)} %len_in.1) | copy-start | bytes 52

commit v4 on v3

--- a/solution.py
+++ b/solution.py
@@ -192,6 +192,9 @@
         gather2(k).start()
 
 
+    loads[2].wait()
+    pt_s[...] = (iota((ROWS, ROWS), 0) == token_of(iota((ROWS, ROWS), 1), g)).astype(F32).astype(BF16)
+    qa, qb, _ = levels_of(q_ref[...])
     for k in range(1, 4):
         gather3(k).wait()
     for k in range(1, 8):
@@ -201,9 +204,6 @@
     send_d = remote(d_ref, doth, one_send.at[0], one_recv.at[0], across)
     send_d.start()
 
-    loads[2].wait()
-    pt_s[...] = (iota((ROWS, ROWS), 0) == token_of(iota((ROWS, ROWS), 1), g)).astype(F32).astype(BF16)
-    qa, qb, _ = levels_of(q_ref[...])
     qx1[...] = stacked(qa, 128)
     qx2[...] = stacked(qb, 32)
     kt_s[...] = tn(k_ref[...], pt_s[...]).astype(BF16)

time: 50 us -> 50 us (level)
  no operation moved by 1% of the time
where the time goes in v4:
time: 50 us; the launch traced here: 49.9 us
  Pallas kernels  48.4 us (97%)
  between operations  0.81 us (2%)
  local copies, waits for them, and re-layouts  0.65 us (1%)
    pallas_call x1, Pallas kernels, shards(): pl.pallas_call(kernel, out_shape=[shape((ROWS, WIDE), BF16)] * 4 + [shape...  46.6 us
    pallas_call x1, Pallas kernels, shards(): pl.pallas_call(finish, out_shape=[shape((ROWS, WIDE), BF16)] * 4 + [shape...  1.78 us

profile of v4, /device:TPU:1, one launch (start us, length us, event | category | flops | bytes accessed | tf_op | source)
XLA Modules:
  0.0 49.9 jit_solution(10228690500628350690)
XLA Ops:
  0.6 0.0 copy-start
  0.6 0.6 %copy-done = s32[4]{0:T(128)S(1)} copy-done((s32[4]{0:T(128)S(1)}, s32[4]{0:T(128)}, u32[]{:S(2)}) %copy-start) | copy-done | bytes 40
  1.3 46.6 %shard_map.101 = (bf16[512,384]{1,0:T(8,128)(2,1)S(1)}, bf16[512,384]{1,0:T(8,128)(2,1)S(1)}, bf16[512,384]{1,0:T(8,128)(2,1)S(1)}, bf16[512,384]{1,0:T(8,128)(2,1)S(1)}, f32[16,384]{1,0:T(8,128)S(1)}) custom-call(bf16[512,384]{1,0:T(8,128)(2,1)} %q_in.1, bf16[512,384]{1,0:T(8,128)(2,1)} %k_in.1, bf16[512,384]{1,0:T(8,128)(2,1)} %v_in.1, ...), custom_call_target="tpu_custom_call" | custom-call | tf_op jit(solution)/shard_map/pallas_call | solution.py:610
  47.9 1.8 %shard_map.102 = (bf16[512,384]{1,0:T(8,128)(2,1)}, bf16[512,384]{1,0:T(8,128)(2,1)}, bf16[512,384]{1,0:T(8,128)(2,1)}, bf16[512,384]{1,0:T(8,128)(2,1)}, f32[12,384]{1,0:T(8,128)}) custom-call(bf16[512,384]{1,0:T(8,128)(2,1)S(1)} %get-tuple-element.15.a, bf16[512,384]{1,0:T(8,128)(2,1)S(1)} %get-tuple-element.16.b, ...), custom_call_target="tpu_custom_call" | custom-call | tf_op jit(solution)/shard_map/pallas_call | solution.py:620
Async XLA Ops:
  0.6 0.7 %copy-start = (s32[4]{0:T(128)S(1)}, s32[4]{0:T(128)}, u32[]{:S(2)}) copy-start(s32[4]{0:T(128)} %len_in.1) | copy-start | bytes 52
